TPU v7x, 256 devices: a whole 4x4x8 slice. The times are simulated.
256 devices in a mesh: row: 8 (over x_hi, y), col: 32 (over x_lo, z, core).
Axes of the slice: x: 4 (x_hi: 2, x_lo: 2; x = x_hi * 2 + x_lo), y: 4, z: 8, core: 2. Of those that a mesh axis runs over, the one named last changes fastest.
Arguments:
- out_grad: bfloat16 [32768, 512], P('col', 'row'), may hold values from -6 to 6
- node_in: bfloat16 [32768, 512], P(('row', 'col')), may hold values from -0.03125 to 0.03125
- weights: bfloat16 [3, 512, 512], replicated, may hold values from -0.25 to 0.25
- tile_vals: bfloat16 [3, 32, 8, 32, 128, 128], P(None, 'col', 'row'), may hold values from -0.15625 to 0.15625
- tile_rows: int32 [3, 32, 8, 32], P(None, 'col', 'row'), may hold values from 0 to 7
- tile_cols: int32 [3, 32, 8, 32], P(None, 'col', 'row'), may hold values from 0 to 31
- tile_count: int32 [3, 32, 8], P(None, 'col', 'row'), may hold values from 1 to 32, as said below
Outputs:
- d_nodes: bfloat16 [32768, 512], P(('row', 'col'))
- d_weights: float32 [3, 512, 512], replicated
Inputs may be any that keep to these rules, and one draw needn't show every extreme that they name: Only the first tile_count slots of a block's list hold tiles; later slots are ignored. In every relation some block uses all 32 slots. `tile_rows`: coordinates may repeat within a block's list; such tiles add.
All inputs are finite; a program needn't handle non-finite values.
Results may differ from a plain program's by a relative error of at most 0.005.
Values may be sent and summed in bfloat16 or wider, within the bound.
A program may use at most 256 MiB of HBM per device.

v0:
```python
import functools

import jax
import jax.numpy as jnp
from jax import lax
from jax.experimental import pallas as pl
from jax.experimental.pallas import tpu as pltpu
from jax.sharding import PartitionSpec as P

MESH = pl.DeviceIdType.MESH
F32 = jnp.float32
BF16 = jnp.bfloat16


def assemble_kernel(rows_ref, cols_ref, count_ref, tiles_ref, out_ref, total):
    relation = pl.program_id(0)
    tile_rows, tile_cols, tile = total.shape[0], total.shape[1], total.shape[2]
    for i in range(tile_rows):
        for j in range(tile_cols):
            total[i, j] = jnp.zeros((tile, tile), F32)

    def add_tile(slot, carry):
        i = rows_ref[relation, 0, 0, slot]
        j = cols_ref[relation, 0, 0, slot]
        total[i, j] = total[i, j] + tiles_ref[0, slot].astype(F32)
        return carry

    lax.fori_loop(0, count_ref[relation], add_tile, 0)
    for i in range(tile_rows):
        for j in range(tile_cols):
            out_ref[i * tile : (i + 1) * tile, j * tile : (j + 1) * tile] = total[i, j].astype(BF16)


def assemble(tile_vals, tile_rows, tile_cols, tile_count, targets, sources):
    relations, cap, tile = tile_vals.shape[0], tile_vals.shape[3], tile_vals.shape[4]
    vals = tile_vals.reshape(relations, cap, tile, tile)
    return pl.pallas_call(
        assemble_kernel,
        grid_spec=pltpu.PrefetchScalarGridSpec(
            num_scalar_prefetch=3,
            grid=(relations,),
            in_specs=[pl.BlockSpec((1, cap, tile, tile), lambda r, *_: (r, 0, 0, 0))],
            out_specs=pl.BlockSpec((targets, sources), lambda r, *_: (r, 0)),
            scratch_shapes=[pltpu.VMEM((targets // tile, sources // tile, tile, tile), F32)],
        ),
        out_shape=jax.ShapeDtypeStruct((relations * targets, sources), BF16),
        compiler_params=pltpu.CompilerParams(vmem_limit_bytes=60 * 2**20),
    )(
        tile_rows,
        tile_cols,
        tile_count.reshape(relations),
        vals,
    )


def main_kernel(
    nr, nc, relations,
    grad_ref, nodes_ref, w_hbm, a_hbm,
    dn_ref, ag_ref,
    gslot, g, w, a, xall, pt, nsend, nrecv, ncomb, ndst,
    dw, dwrecv, pbuf, precv, zbuf, zrecv,
    load_sem, gs, gr, xs, xr, fs, fr, ns, nrs, nzs, nzr, ds, dr, ps, pr, zs, zr,
    azs, azr, aps, apr, acs, acr,
):
    nz = nc // 2
    tn = grad_ref.shape[0]
    width = grad_ref.shape[1]
    nd = nodes_ref.shape[0]
    f = w_hbm.shape[1]
    me_r = lax.axis_index("row")
    me_c = lax.axis_index("col")
    z = me_c // 2
    core = me_c % 2
    other = 1 - core
    sibling = {"col": z * 2 + other}

    def row_peer(d):
        return {"row": lax.rem(me_r + d, nr)}

    def z_peer(d):
        return {"col": lax.rem(z + d, nz) * 2 + core}

    def remote(src, dst, send, recv, dev):
        return pltpu.make_async_remote_copy(
            src_ref=src, dst_ref=dst, send_sem=send, recv_sem=recv, device_id=dev, device_id_type=MESH
        )

    def x_slot(k):
        return xall.at[pl.ds(pl.multiple_of(k * nd, nd), nd), :]

    load_a = pltpu.make_async_copy(a_hbm, a, load_sem.at[0])
    load_w = pltpu.make_async_copy(w_hbm, w, load_sem.at[1])
    load_w.start()
    load_a.start()

    barrier = pltpu.get_barrier_semaphore()
    for d in range(1, nr):
        pl.semaphore_signal(barrier, inc=1, device_id=row_peer(d), device_id_type=MESH)
    for d in range(1, nz):
        pl.semaphore_signal(barrier, inc=1, device_id=z_peer(d), device_id_type=MESH)
    pl.semaphore_signal(barrier, inc=1, device_id=sibling, device_id_type=MESH)
    pl.semaphore_wait(barrier, nr - 1 + nz - 1 + 1)

    g_copies = [
        remote(grad_ref, gslot.at[me_r], gs.at[d - 1], gr.at[d - 1], row_peer(d)) for d in range(1, nr)
    ]
    for c in g_copies:
        c.start()
    x_copies = [
        remote(nodes_ref, x_slot(me_c), xs.at[d - 1], xr.at[d - 1], z_peer(d)) for d in range(1, nz)
    ]
    for c in x_copies:
        c.start()
    f_copies = [remote(nodes_ref, x_slot(me_c), fs.at[0], fr.at[0], sibling)]
    f_copies[0].start()
    xall[pl.ds(pl.multiple_of(me_c * nd, nd), nd), :] = nodes_ref[...]
    gslot[me_r] = grad_ref[...]

    load_w.wait()
    for c in g_copies:
        c.wait_recv()
    for k in range(nr):
        g[:, k * width : (k + 1) * width] = gslot[k]
    for r in range(relations):
        pt[:, r * tn : (r + 1) * tn] = lax.dot_general(
            w[r], g[...], (((1,), (1,)), ((), ())), preferred_element_type=F32
        ).astype(BF16)
    load_a.wait()

    def mix(k, carry):
        cols = pl.ds(pl.multiple_of(k * 2 * nd, 2 * nd), 2 * nd)
        both = jnp.dot(pt[...], a[:, cols], preferred_element_type=F32)
        nsend[0, k] = both[:, :nd]
        nsend[1, k] = both[:, nd:]
        return carry

    lax.fori_loop(0, nz, mix, 0)
    n_core = remote(nsend.at[other], nrecv, ns.at[0], nrs.at[0], sibling)
    n_core.start()

    for d in range(1, nz):
        x_copies[d - 1].wait_recv()
        slot = lax.rem(z + nz - d, nz) * 2 + core
        c = remote(x_slot(slot), x_slot(slot), fs.at[d], fr.at[d], sibling)
        c.start()
        f_copies.append(c)

    n_core.wait_recv()

    def combine(k, carry):
        ncomb[k] = (nsend[core, k] + nrecv[k]).astype(BF16)
        return carry

    lax.fori_loop(0, nz, combine, 0)
    n_copies = [
        remote(ncomb.at[lax.rem(z + d, nz)], ndst.at[d - 1], nzs.at[d - 1], nzr.at[d - 1], z_peer(d))
        for d in range(1, nz)
    ]
    for c in n_copies[:-1]:
        c.start()

    for c in f_copies:
        c.wait_recv()

    chunk = f // 2
    plane_rows = pbuf.shape[2]
    piece = zbuf.shape[2]
    sent = [[] for _ in range(relations)]
    batches = [[None] * relations for _ in range(5)]

    def launch(stage, r, copies):
        for c in copies:
            c.start()
        batches[stage][r] = copies
        sent[r].extend(copies)

    def arrived(stage, r):
        for c in batches[stage][r]:
            c.wait_recv()

    def terms(r):
        for h in range(2):
            y = jnp.dot(
                a[r * tn : (r + 1) * tn, :],
                xall[:, h * chunk : (h + 1) * chunk],
                preferred_element_type=F32,
            )
            dw[r, h] = jnp.dot(y.astype(BF16).T, g[...], preferred_element_type=F32)
        launch(0, r, [remote(dw.at[r, other], dwrecv.at[r], ds.at[r, 0], dr.at[r, 0], sibling)])

    def plane_scatter(r):
        arrived(0, r)
        for k in range(nr):
            rows = slice(k * plane_rows, (k + 1) * plane_rows)
            pbuf[r, k] = (dw[r, core, rows, :] + dwrecv[r, rows, :]).astype(BF16)
        launch(1, r, [
            remote(
                pbuf.at[r, lax.rem(me_r + d, nr)], precv.at[r, d - 1],
                ps.at[r, d - 1], pr.at[r, d - 1], row_peer(d),
            )
            for d in range(1, nr)
        ])

    def z_scatter(r):
        arrived(1, r)
        for k in range(nz):
            rows = slice(k * piece, (k + 1) * piece)
            part = pbuf[r, me_r, rows, :].astype(F32)
            for d in range(1, nr):
                part = part + precv[r, d - 1, rows, :].astype(F32)
            zbuf[r, k] = part.astype(BF16)
        launch(2, r, [
            remote(
                zbuf.at[r, lax.rem(z + d, nz)], zrecv.at[r, d - 1],
                zs.at[r, d - 1], zr.at[r, d - 1], z_peer(d),
            )
            for d in range(1, nz)
        ])

    def z_gather(r):
        arrived(2, r)
        final = zbuf[r, z].astype(F32)
        for d in range(1, nz):
            final = final + zrecv[r, d - 1].astype(F32)
        ag_ref[r, core, me_r, z] = final.astype(BF16)
        mine = ag_ref.at[r, core, me_r, z]
        launch(3, r, [remote(mine, mine, azs.at[r, d - 1], azr.at[r, d - 1], z_peer(d)) for d in range(1, nz)])

    last = [[] for _ in range(relations)]

    def plane_gather(r):
        arrived(3, r)
        mine = ag_ref.at[r, core, me_r]
        launch(4, r, [remote(mine, mine, aps.at[r, d - 1], apr.at[r, d - 1], row_peer(d)) for d in range(1, nr)])
        c = remote(mine, mine, acs.at[r, 0], acr.at[r, 0], sibling)
        c.start()
        last[r].append(c)

    def core_gather(r):
        for d in range(1, nr):
            batches[4][r][d - 1].wait_recv()
            slot = ag_ref.at[r, core, lax.rem(me_r + nr - d, nr)]
            c = remote(slot, slot, acs.at[r, d], acr.at[r, d], sibling)
            c.start()
            last[r].append(c)

    terms(0)
    for r in range(1, relations):
        terms(r)
        plane_scatter(r - 1)
    plane_scatter(relations - 1)
    stages = (z_scatter, z_gather, plane_gather, core_gather)
    for t in range(relations + len(stages) - 1):
        for stage in range(len(stages)):
            if 0 <= t - stage < relations:
                stages[stage](t - stage)
        if t == relations:
            n_copies[-1].start()

    for c in n_copies:
        c.wait_recv()
    own = nsend[core, z] + nrecv[z]
    for d in range(1, nz):
        own = own + ndst[d - 1].astype(F32)
    dn_ref[...] = own.T.astype(BF16)

    for r in range(relations):
        for c in last[r]:
            c.wait_recv()
        for c in sent[r] + last[r]:
            c.wait_send()
    for c in g_copies + x_copies + f_copies + [n_core] + n_copies:
        c.wait_send()


def widen_kernel(dn_ref, dw_ref, dn_out, dw_out, nodes, narrow, wide, in_sem, out_sem):
    parts, rows = narrow.shape[0], narrow.shape[1]

    def part(ref, k):
        return ref.at[k * rows : (k + 1) * rows, :]

    loads = [pltpu.make_async_copy(part(dw_ref, k), narrow.at[k], in_sem.at[k]) for k in range(parts)]
    stores = [pltpu.make_async_copy(wide.at[k], part(dw_out, k), out_sem.at[k]) for k in range(parts)]
    loads.append(pltpu.make_async_copy(dn_ref, nodes, in_sem.at[parts]))
    stores.append(pltpu.make_async_copy(nodes, dn_out, out_sem.at[parts]))
    for c in loads:
        c.start()
    for k in range(parts):
        loads[k].wait()
        wide[k] = narrow[k].astype(F32)
        stores[k].start()
    loads[parts].wait()
    stores[parts].start()
    for c in stores:
        c.wait()


def widen(d_nodes, gathered):
    total, f = gathered.shape
    parts = 6 if total % 96 == 0 else 1
    rows = total // parts
    hbm = pl.BlockSpec(memory_space=pltpu.HBM)
    return pl.pallas_call(
        widen_kernel,
        in_specs=[hbm, hbm],
        out_specs=(hbm, hbm),
        out_shape=(
            jax.ShapeDtypeStruct(d_nodes.shape, BF16),
            jax.ShapeDtypeStruct(gathered.shape, F32),
        ),
        scratch_shapes=[
            pltpu.VMEM(d_nodes.shape, BF16),
            pltpu.VMEM((parts, rows, f), BF16),
            pltpu.VMEM((parts, rows, f), F32),
            pltpu.SemaphoreType.DMA((parts + 1,)),
            pltpu.SemaphoreType.DMA((parts + 1,)),
        ],
    )(d_nodes, gathered)


def body(nr, nc, out_grad, node_in, weights, tile_vals, tile_rows, tile_cols, tile_count):
    relations, f = weights.shape[0], weights.shape[1]
    tn, width = out_grad.shape
    nd = node_in.shape[0]
    sn = nd * nc
    nz = nc // 2
    half = f // 2
    plane_rows = half // nr
    piece = plane_rows // nz
    dense = assemble(tile_vals, tile_rows, tile_cols, tile_count, tn, sn)
    dma = lambda *n: pltpu.SemaphoreType.DMA(n)
    vmem = pl.BlockSpec(memory_space=pltpu.VMEM)
    hbm = pl.BlockSpec(memory_space=pltpu.HBM)
    d_nodes, gathered = pl.pallas_call(
        functools.partial(main_kernel, nr, nc, relations),
        out_shape=(
            jax.ShapeDtypeStruct((nd, f), BF16),
            jax.ShapeDtypeStruct((relations, 2, nr, nz, piece, f), BF16),
        ),
        in_specs=[vmem, vmem, hbm, hbm],
        out_specs=(vmem, vmem),
        scratch_shapes=[
            pltpu.VMEM((nr, tn, width), BF16),
            pltpu.VMEM((tn, f), BF16),
            pltpu.VMEM(weights.shape, BF16),
            pltpu.VMEM((relations * tn, sn), BF16),
            pltpu.VMEM((sn, f), BF16),
            pltpu.VMEM((f, relations * tn), BF16),
            pltpu.VMEM((2, nz, f, nd), F32),
            pltpu.VMEM((nz, f, nd), F32),
            pltpu.VMEM((nz, f, nd), BF16),
            pltpu.VMEM((nz - 1, f, nd), BF16),
            pltpu.VMEM((relations, 2, half, f), F32),
            pltpu.VMEM((relations, half, f), F32),
            pltpu.VMEM((relations, nr, plane_rows, f), BF16),
            pltpu.VMEM((relations, nr - 1, plane_rows, f), BF16),
            pltpu.VMEM((relations, nz, piece, f), BF16),
            pltpu.VMEM((relations, nz - 1, piece, f), BF16),
            dma(2),
            dma(nr - 1), dma(nr - 1),
            dma(nz - 1), dma(nz - 1),
            dma(nz), dma(nz),
            dma(1), dma(1),
            dma(nz - 1), dma(nz - 1),
            dma(relations, 1), dma(relations, 1),
            dma(relations, nr - 1), dma(relations, nr - 1),
            dma(relations, nz - 1), dma(relations, nz - 1),
            dma(relations, nz - 1), dma(relations, nz - 1),
            dma(relations, nr - 1), dma(relations, nr - 1),
            dma(relations, nr), dma(relations, nr),
        ],
        compiler_params=pltpu.CompilerParams(
            collective_id=0, has_side_effects=True, vmem_limit_bytes=67043328
        ),
    )(out_grad, node_in, weights, dense)
    d_nodes, d_weights = widen(d_nodes, gathered.reshape(relations * f, f))
    return d_nodes, d_weights.reshape(relations, f, f)


def solution(mesh):
    return jax.shard_map(
        functools.partial(body, mesh.shape["row"], mesh.shape["col"]),
        mesh=mesh,
        in_specs=(
            P("col", "row"),
            P(("row", "col"), None),
            P(),
            P(None, "col", "row", None, None, None),
            P(None, "col", "row", None),
            P(None, "col", "row", None),
            P(None, "col", "row"),
        ),
        out_specs=(P(("row", "col"), None), P()),
        check_vma=False,
    )
```

profile of v0, /device:TPU:1, one launch (start us, length us, event | category | flops | bytes accessed | tf_op | source)
XLA Modules:
  0.0 182.2 jit_solution(5079305635552774396)
XLA Ops:
  0.6 1.7 copy.9.grad_ref
  2.4 14.2 %shard_map.86.a_hbm = bf16[3072,4096]{1,0:T(8,128)(2,1)} custom-call(s32[3,1,1,32]{3,2,1,0:T(1,128)} %rows_ref.1, s32[3,1,1,32]{3,2,1,0:T(1,128)} %cols_ref.1, s32[3]{0:T(128)} %bitcast.4, bf16[3,32,128,128]{3,2,1,0:T(8,128)(2,1)} %bitcast.3), custom_call_target="tpu_custom_call" | custom-call | tf_op jit(solution)/shard_map/pallas_call | solution.py:37
  16.6 158.9 %shard_map.87 = (bf16[128,512]{1,0:T(8,128)(2,1)}, bf16[3,2,8,16,2,512]{5,4,3,2,1,0:T(2,128)(2,1)}) custom-call(bf16[1024,64]{1,0:T(8,128)(2,1)} %copy.9.grad_ref, bf16[128,512]{1,0:T(8,128)(2,1)} %nodes_ref.1, bf16[3,512,512]{2,1,0:T(8,128)(2,1)} %w_hbm.1, bf16[3072,4096]{1,0:T(8,128)(2,1)} %shard_map.86.a_hbm), custom_call_target="tpu_custom_call" | custom-call | tf_op jit(solution)/shard_map/pallas_call | solution.py:334
  175.5 3.6 %reshape.18.dw_ref = bf16[1536,512]{1,0:T(8,128)(2,1)} reshape(bf16[3,2,8,16,2,512]{5,4,3,2,1,0:T(2,128)(2,1)} %get-tuple-element.7) | data formatting | bytes 3145728 | tf_op jit(solution)/shard_map/reshape | solution.py:376
  179.2 2.8 %shard_map.88 = (bf16[128,512]{1,0:T(8,128)(2,1)}, f32[1536,512]{1,0:T(8,128)}) custom-call(bf16[128,512]{1,0:T(8,128)(2,1)} %get-tuple-element.6.dn_ref, bf16[1536,512]{1,0:T(8,128)(2,1)} %reshape.18.dw_ref), custom_call_target="tpu_custom_call" | custom-call | tf_op jit(solution)/shard_map/pallas_call | solution.py:303
where the time goes:
time: 182 us
  Pallas kernels  176 us (97%)
  local copies, waits for them, and re-layouts  5.39 us (3%)
    pallas_call x1, Pallas kernels, body(): pl.pallas_call(functools.partial(main_kernel, nr, nc, relations), out_sha...  159 us
    pallas_call x1, Pallas kernels, assemble(): pl.pallas_call(assemble_kernel, grid_spec=pltpu.PrefetchScalarGridSpec(nu...  14.2 us
    reshape x1, local copies, waits for them, and re-layouts, body(): d_nodes, d_weights = widen(d_nodes, gathered.reshape(relations * f, f))  3.65 us

commit v1 on v0

v1 whole, which is shorter than its diff:
```python
import functools

import jax
import jax.numpy as jnp
from jax import lax
from jax.experimental import pallas as pl
from jax.experimental.pallas import tpu as pltpu
from jax.sharding import PartitionSpec as P

MESH = pl.DeviceIdType.MESH
F32 = jnp.float32
BF16 = jnp.bfloat16
SEMS = 360


def main_kernel(
    nr, nc, relations, cap,
    gin_ref, nodes_ref, rows_s, cols_s, count_s, rows_v, cols_v, w_hbm, t_hbm,
    dn_ref, ag_ref,
    gt, gy, w, tiles, tilest, xall, pm, acc, nsend, nrecv, nown, meta, link,
    zsa, zra, zsb, zrb, xs, xr, xf, dwrecv, pbuf, precv, zbuf, zrecv,
    load_sem, ssem, rsem,
):
    ny = nr // 2
    nz = nc // 4
    nk = nc // 2
    nd, f = nodes_ref.shape
    gb, tn = gin_ref.shape
    nt = tn // nd
    half = f // 2
    hb = half // nd
    me_r = lax.axis_index("row")
    me_c = lax.axis_index("col")
    xh = me_r // ny
    y = lax.rem(me_r, ny)
    xl = me_c // (2 * nz)
    z = lax.rem(me_c // 2, nz)
    core = lax.rem(me_c, 2)
    other = 1 - core

    def zat(dz):
        return lax.rem(z + (dz + 2 * nz), nz)

    def kat(x, zz):
        return x * nz + zz

    def cat(x, zz):
        return kat(x, zz) * 2 + core

    sibling = {"col": kat(xl, z) * 2 + other}
    xdev = {"col": cat(1 - xl, z)}
    xhdev = {"row": (1 - xh) * ny + y}

    def zdev(dz):
        return {"col": cat(xl, zat(dz))}

    def yat(dy):
        return lax.rem(y + (dy + 2 * ny), ny)

    def ydev(dy):
        return {"row": xh * ny + yat(dy)}

    def row_peer(d):
        r = lax.rem(me_r + d, nr)
        side = lax.rem(xl + xh + r // ny, 2)
        return {"row": r, "col": cat(side, z)}

    def k_peer(d):
        k = lax.rem(kat(xl, z) + d, nk)
        return k, {"col": k * 2 + core}

    used = [0]
    started = []

    def send(src, dst, dev):
        i = used[0]
        used[0] += 1
        c = pltpu.make_async_remote_copy(
            src_ref=src, dst_ref=dst, send_sem=ssem.at[i], recv_sem=rsem.at[i],
            device_id=dev, device_id_type=MESH,
        )
        c.start()
        started.append(c)
        return c

    load_w = pltpu.make_async_copy(w_hbm, w, load_sem.at[0])
    load_t = pltpu.make_async_copy(t_hbm, tiles, load_sem.at[1])
    load_t.start()
    load_w.start()

    barrier = pltpu.get_barrier_semaphore()
    for d in range(1, nr):
        pl.semaphore_signal(barrier, inc=1, device_id=row_peer(d), device_id_type=MESH)
    for d in range(1, nk):
        pl.semaphore_signal(barrier, inc=1, device_id=k_peer(d)[1], device_id_type=MESH)
    pl.semaphore_signal(barrier, inc=1, device_id=sibling, device_id_type=MESH)
    pl.semaphore_signal(barrier, inc=1, device_id=xhdev, device_id_type=MESH)
    pl.semaphore_wait(barrier, nr - 1 + nk - 1 + 2)

    def hops(n, orient, way):
        return n // 2 if way == orient else n - 1 - n // 2

    gh = gb // 2
    g_streams = {"o0": (0, 1), "o1": (1, -1), "p0": (0, 1), "p1": (1, -1)}

    def g_ref(st, dy):
        side = xh if st[0] == "o" else 1 - xh
        row = (side * ny + yat(dy)) * gb + g_streams[st][0] * gh
        return gt.at[pl.ds(pl.multiple_of(row, gh), gh), :]

    gcopy = {}

    def g_send(st, way, h):
        here = g_ref(st, -way * (h - 1))
        src = gin_ref.at[pl.ds(g_streams[st][0] * gh, gh), :] if h == 1 and st[0] == "o" else here
        gcopy[st, way, h] = send(src, here, ydev(way))

    def g_first(st):
        for way in (1, -1):
            if hops(ny, g_streams[st][1], way) >= 1:
                g_send(st, way, 1)

    def g_arrive(st, way, h):
        if (st, way, h) not in gcopy:
            return
        gcopy[st, way, h].wait_recv()
        if h < hops(ny, g_streams[st][1], way):
            g_send(st, way, h + 1)

    q = nd // 4
    x_streams = {"b0": (2 * q, q, 1), "b1": (3 * q, q, -1), "own": (0, 2 * q, 1), "par": (0, 2 * q, -1)}

    def x_rows(st):
        return slice(x_streams[st][0], x_streams[st][0] + x_streams[st][1])

    def x_ref(st, dz, x=None):
        if x is None:
            x = 1 - xl if st == "par" else xl
        return xall.at[cat(x, zat(dz)), x_rows(st), :]

    xcopy = {}
    xfwd = {}
    sib = []

    def to_sibling(ref):
        sib.append(send(ref, ref, sibling))

    def x_send(st, way, h):
        here = x_ref(st, -way * (h - 1))
        src = nodes_ref.at[x_rows(st), :] if h == 1 and st != "par" else here
        xcopy[st, way, h] = send(src, here, zdev(way))

    def x_first(st):
        for way in (1, -1):
            if hops(nz, x_streams[st][2], way) >= 1:
                x_send(st, way, 1)

    def x_arrive(st, way, h):
        if (st, way, h) not in xcopy:
            return
        xcopy[st, way, h].wait_recv()
        if h < hops(nz, x_streams[st][2], way):
            x_send(st, way, h + 1)
        here = x_ref(st, -way * h)
        if st[0] == "b":
            xfwd[st, way, h] = send(here, here, xdev)
        to_sibling(here)

    def x_cross(st, way, h):
        if (st, way, h) not in xfwd:
            return
        xfwd[st, way, h].wait_recv()
        to_sibling(x_ref(st, -way * h, 1 - xl))

    mine = xall.at[me_c]
    swap = send(nodes_ref.at[x_rows("par"), :], mine.at[x_rows("par"), :], xdev)
    for st in ("o0", "o1"):
        g_first(st)
    gswap = send(gin_ref, gt.at[pl.ds(pl.multiple_of(me_r * gb, gb), gb), :], xhdev)
    for st in ("b0", "b1", "own"):
        x_first(st)
    for st in ("b0", "b1"):
        xfwd[st, 0, 0] = send(nodes_ref.at[x_rows(st), :], mine.at[x_rows(st), :], xdev)
    sib.append(send(nodes_ref, mine, sibling))
    xall[me_c] = nodes_ref[...]
    gt[pl.ds(pl.multiple_of(me_r * gb, gb), gb), :] = gin_ref[...]

    slot_row = lax.broadcasted_iota(jnp.int32, (cap, cap), 0)
    slot_col = lax.broadcasted_iota(jnp.int32, (cap, cap), 1)
    places = lax.broadcasted_iota(jnp.int32, (cap, nc), 1)
    numbers = lax.broadcasted_iota(jnp.int32, (cap, nc), 0)

    def keys(ref, r):
        lane = lax.broadcasted_iota(jnp.int32, (1, cap), 1)
        key = jnp.where(lane < count_s[r], ref[r, 0], -1)
        turned = jnp.max(jnp.where(slot_row == slot_col, jnp.broadcast_to(key, (cap, cap)), -1), axis=1, keepdims=True)
        return key, turned

    def before(turned, key, offset, whole):
        same = turned == key
        if not whole:
            same = same & (slot_row < slot_col)
        return jnp.max(jnp.where(same, slot_row + (1 + offset), 0), axis=0, keepdims=True)

    def final(turned, offset):
        return jnp.max(jnp.where(turned == places, numbers + (1 + offset), 0), axis=0, keepdims=True)

    by_col = [keys(cols_v, r) for r in range(relations)]
    ends = final(by_col[0][1], 0)
    for r in range(1, relations):
        ends = jnp.maximum(ends, final(by_col[r][1], r * cap))
    meta[relations : relations + 1, 0:nc] = ends
    for r in range(relations):
        prior = before(by_col[r][1], by_col[r][0], r * cap, False)
        for e in range(r):
            prior = jnp.maximum(prior, before(by_col[e][1], by_col[r][0], e * cap, True))
        meta[r : r + 1, 0:cap] = prior
        key, turned = keys(rows_v, r)
        meta[4 + r : 5 + r, 0:cap] = before(turned, key, 0, False)
        meta[8 + r : 9 + r, 0:nc] = final(turned, 0)
    to_scalar = pltpu.make_async_copy(meta, link, load_sem.at[2])
    to_scalar.start()

    load_t.wait()

    def turn(r):
        def one(s, carry):
            tilest[r * cap + s] = tiles[r * cap + s].T
            return carry

        lax.fori_loop(0, cap, one, 0, unroll=4)

    turn(0)
    swap.wait_recv()
    to_sibling(x_ref("par", 0))
    x_first("par")
    gswap.wait_recv()
    for st in ("p0", "p1"):
        g_first(st)
    for way in (1, -1):
        for st in ("o0", "o1"):
            g_arrive(st, way, 1)
    turn(1)

    def x_round(h):
        for st in ("b0", "b1", "own", "par"):
            for way in (1, -1):
                x_arrive(st, way, h)
        for st in ("b0", "b1"):
            if h == 1:
                x_cross(st, 0, 0)
            for way in (1, -1):
                x_cross(st, way, h - 1)

    x_round(1)
    turn(2)
    for way in (1, -1):
        for st in ("p0", "p1"):
            g_arrive(st, way, 1)
    x_round(2)
    for h in range(2, ny):
        for way in (1, -1):
            for st in g_streams:
                g_arrive(st, way, h)
    load_w.wait()
    x_round(3)
    to_scalar.wait()

    for b in range(f // nd):
        gy[:, b * nd : (b + 1) * nd] = gt[b * nd : (b + 1) * nd, :].T
    for r in range(relations):
        prod = lax.dot_general(
            gy[...], w[r], (((1,), (1,)), ((), ())), preferred_element_type=F32
        ).astype(BF16)
        for i in range(nt):
            pm[r * nt + i] = prod[i * nd : (i + 1) * nd, :]
    acc[0] = jnp.zeros((nd, f), F32)

    def mix(r):
        def one(s, carry):
            t = r * cap + s
            p = jnp.dot(tilest[t], pm[r * nt + rows_s[r, 0, 0, s]], preferred_element_type=F32)
            acc[t + 1] = p + acc[link[r, s]]
            return carry

        lax.fori_loop(0, cap, one, 0, unroll=4)

    mix(0)
    mix(1)
    x_round(4)
    mix(2)

    order = [nz // 2]
    for d in range(nz // 2 - 1, 0, -1):
        order += [d, -d]
    order.append(0)
    ncore = {}
    for dz in order:
        for x in (0, 1):
            k = kat(1 - xl if x == 0 else xl, zat(dz))
            nsend[k] = acc[link[relations, 2 * k + other]]
            ncore[dz, x] = send(nsend.at[k], nrecv.at[k], sibling)

    xcross = {}

    def n_core(dz):
        for x in (0, 1):
            ncore[dz, x].wait_recv()
            k = kat(1 - xl if x == 0 else xl, zat(dz))
            nown[k] = nown[k] + nrecv[k]
        slot = zat(dz)
        xs[slot] = nown[kat(1 - xl, slot), 2 * q :, :].astype(BF16)
        xcross[dz] = send(xs.at[slot], xr.at[slot], xdev)

    def n_cross(dz):
        xcross[dz].wait_recv()
        k = kat(xl, zat(dz))
        nown[k, 2 * q :, :] = nown[k, 2 * q :, :] + xr[zat(dz)].astype(F32)

    zcopy = {}
    parts = {"par": (zsa, zra, 0), "own": (zsa, zra, 1), "b0": (zsb, zrb, 0), "b1": (zsb, zrb, 1)}

    def n_send(st, way, t):
        n = hops(nz, x_streams[st][2], way)
        if t > n:
            return
        sbuf, rbuf, slot = parts[st]
        side = 0 if way == 1 else 1
        x = 1 - xl if st == "par" else xl
        value = nown[kat(x, zat(way * (n + 1 - t))), x_rows(st), :]
        if t > 1:
            zcopy[st, way, t - 1].wait_recv()
            value = value + rbuf[slot, side, t - 2].astype(F32)
        sbuf[slot, side, t - 1] = value.astype(BF16)
        zcopy[st, way, t] = send(sbuf.at[slot, side, t - 1], rbuf.at[slot, side, t - 1], zdev(way))

    def n_final(st):
        x = 1 - xl if st == "par" else xl
        value = nown[kat(x, z), x_rows(st), :]
        for way in (1, -1):
            n = hops(nz, x_streams[st][2], way)
            if n:
                zcopy[st, way, n].wait_recv()
                _, rbuf, slot = parts[st]
                value = value + rbuf[slot, 0 if way == 1 else 1, n - 1].astype(F32)
        return value

    def n_round(t, names):
        for st in names:
            for way in (1, -1):
                n_send(st, way, t)

    base = cap + 1
    blocks = f // nd

    def terms(r):
        def one(s, carry):
            t = r * cap + s
            p = jnp.dot(tiles[t], xall[cols_s[r, 0, 0, s]], preferred_element_type=F32)
            acc[s + 1] = p + acc[link[4 + r, s]]
            return carry

        lax.fori_loop(0, cap, one, 0, unroll=4)
        for i in range(nt):
            gy[i * nd : (i + 1) * nd, :] = acc[link[8 + r, i]].astype(BF16)

    batches = {}

    def product(r):
        for b in range(blocks):
            acc[base + r * blocks + b] = jnp.dot(
                gt[b * nd : (b + 1) * nd, :], gy[...], preferred_element_type=F32
            )
        src = acc.at[pl.ds(base + r * blocks + other * hb, hb)]
        batches[0, r] = [send(src, dwrecv.at[r], sibling)]

    def arrived(stage, r):
        for c in batches[stage, r]:
            c.wait_recv()

    prow = f // nr

    def plane_scatter(r):
        arrived(0, r)
        for b in range(hb):
            total = acc[base + r * blocks + core * hb + b] + dwrecv[r, b]
            pbuf[r, :, b * nd : (b + 1) * nd] = total.astype(BF16).T
        copies = []
        for d in range(1, nr):
            peer = lax.rem(me_r + d, nr)
            src = pbuf.at[r, pl.ds(pl.multiple_of(peer * prow, prow), prow), :]
            copies.append(send(src, precv.at[r, d - 1], row_peer(d)))
        batches[1, r] = copies

    lanes = half // 128
    zrows = prow * lanes // nz

    def piece(zz):
        row = pl.multiple_of((zz // lanes) * zrows, zrows)
        lane = pl.multiple_of(lax.rem(zz, lanes) * 128, 128)
        return row, lane

    def z_scatter(r):
        arrived(1, r)
        part = pbuf[r, pl.ds(pl.multiple_of(me_r * prow, prow), prow), :].astype(F32)
        for d in range(1, nr):
            part = part + precv[r, d - 1].astype(F32)
        zbuf[r] = part.astype(BF16)
        me_k = kat(xl, z)
        row, lane = piece(z)
        zrecv[r, me_k] = zbuf[r, pl.ds(row, zrows), pl.ds(lane, 128)]
        copies = []
        for d in range(1, nk):
            k, dev = k_peer(d)
            row, lane = piece(lax.rem(k, nz))
            src = zbuf.at[r, pl.ds(row, zrows), pl.ds(lane, 128)]
            copies.append(send(src, zrecv.at[r, me_k], dev))
        batches[2, r] = copies

    def z_gather(r):
        arrived(2, r)
        final = zrecv[r, 0].astype(F32)
        for k in range(1, nk):
            final = final + zrecv[r, k].astype(F32)
        row, lane = piece(z)
        row = pl.multiple_of(r * f + me_r * prow + row, zrows)
        lane = pl.multiple_of(core * half + lane, 128)
        ag_ref[pl.ds(row, zrows), pl.ds(lane, 128)] = final.astype(BF16)
        mine = ag_ref.at[pl.ds(row, zrows), pl.ds(lane, 128)]
        batches[3, r] = [send(mine, mine, zdev(d)) for d in range(1, nz)]

    def strip(r, who):
        row = pl.multiple_of(r * f + who * prow, prow)
        return ag_ref.at[pl.ds(row, prow), pl.ds(pl.multiple_of(core * half, half), half)]

    last = []

    def plane_gather(r):
        arrived(3, r)
        mine = strip(r, me_r)
        batches[4, r] = [send(mine, mine, row_peer(d)) for d in range(1, nr)]
        last.append(send(mine, mine, sibling))

    def core_gather(r):
        for d in range(1, nr):
            batches[4, r][d - 1].wait_recv()
            there = strip(r, lax.rem(me_r + nr - d, nr))
            last.append(send(there, there, sibling))

    first = [d for d in order if abs(d) >= nz // 2 - 1]
    rest = [d for d in order if d not in first]
    a_names, b_names = ("par", "own"), ("b0", "b1")

    def keep(k, carry):
        nown[k] = acc[link[relations, 2 * k + core]]
        return carry

    lax.fori_loop(0, nk, keep, 0)
    for dz in first:
        n_core(dz)
    n_round(1, a_names)
    for h in range(5, nz + 1):
        x_round(h)
    for c in sib:
        c.wait_recv()
    terms(0)
    product(0)
    for dz in rest:
        n_core(dz)
    terms(1)
    product(1)
    plane_scatter(0)
    for dz in first:
        n_cross(dz)
    n_round(1, b_names)
    terms(2)
    product(2)
    plane_scatter(1)
    for dz in rest:
        n_cross(dz)
    plane_scatter(2)
    n_round(2, a_names)
    n_round(2, b_names)
    for r in range(relations):
        z_scatter(r)
    n_round(3, a_names)
    n_round(3, b_names)
    for r in range(relations):
        z_gather(r)
    for t in range(4, nz):
        n_round(t, a_names)
        n_round(t, b_names)
    for r in range(relations):
        plane_gather(r)
    xf[0] = n_final("par").astype(BF16)
    xlast = send(xf.at[0], xf.at[1], xdev)
    for st in b_names:
        dn_ref[x_rows(st), :] = n_final(st).astype(BF16)
    own = n_final("own")
    xlast.wait_recv()
    dn_ref[x_rows("own"), :] = (own + xf[1].astype(F32)).astype(BF16)
    for r in range(relations):
        core_gather(r)
    for c in last:
        c.wait_recv()
    for c in started:
        c.wait_send()
    assert used[0] <= SEMS


def widen_kernel(dn_ref, dw_ref, dn_out, dw_out, nodes, narrow, wide, in_sem, out_sem):
    parts, rows = narrow.shape[0], narrow.shape[1]

    def part(ref, k):
        return ref.at[k * rows : (k + 1) * rows, :]

    loads = [pltpu.make_async_copy(part(dw_ref, k), narrow.at[k], in_sem.at[k]) for k in range(parts)]
    stores = [pltpu.make_async_copy(wide.at[k], part(dw_out, k), out_sem.at[k]) for k in range(parts)]
    loads.append(pltpu.make_async_copy(dn_ref, nodes, in_sem.at[parts]))
    stores.append(pltpu.make_async_copy(nodes, dn_out, out_sem.at[parts]))
    for c in loads:
        c.start()
    for k in range(parts):
        loads[k].wait()
        wide[k] = narrow[k].astype(F32)
        stores[k].start()
    loads[parts].wait()
    stores[parts].start()
    for c in stores:
        c.wait()


def widen(d_nodes, gathered):
    total, f = gathered.shape
    parts = 6 if total % 96 == 0 else 1
    rows = total // parts
    hbm = pl.BlockSpec(memory_space=pltpu.HBM)
    return pl.pallas_call(
        widen_kernel,
        in_specs=[hbm, hbm],
        out_specs=(hbm, hbm),
        out_shape=(
            jax.ShapeDtypeStruct(d_nodes.shape, BF16),
            jax.ShapeDtypeStruct(gathered.shape, F32),
        ),
        scratch_shapes=[
            pltpu.VMEM(d_nodes.shape, BF16),
            pltpu.VMEM((parts, rows, f), BF16),
            pltpu.VMEM((parts, rows, f), F32),
            pltpu.SemaphoreType.DMA((parts + 1,)),
            pltpu.SemaphoreType.DMA((parts + 1,)),
        ],
    )(d_nodes, gathered)


def body(nr, nc, out_grad, node_in, weights, tile_vals, tile_rows, tile_cols, tile_count):
    relations, f = weights.shape[0], weights.shape[1]
    tn, width = out_grad.shape
    nd = node_in.shape[0]
    cap, tile = tile_vals.shape[3], tile_vals.shape[4]
    slots = relations * cap
    nt, nz, nk = tn // nd, nc // 4, nc // 2
    half = f // 2
    hb = half // nd
    prow = f // nr
    q = nd // 4
    hop = max(nz // 2, 1)
    zrows = prow * (half // 128) // nz

    dma = lambda *n: pltpu.SemaphoreType.DMA(n)
    vmem = pl.BlockSpec(memory_space=pltpu.VMEM)
    smem = pl.BlockSpec(memory_space=pltpu.SMEM)
    hbm = pl.BlockSpec(memory_space=pltpu.HBM)
    d_nodes, gathered = pl.pallas_call(
        functools.partial(main_kernel, nr, nc, relations, cap),
        out_shape=(
            jax.ShapeDtypeStruct((nd, f), BF16),
            jax.ShapeDtypeStruct((relations * f, f), BF16),
        ),
        in_specs=[vmem, vmem, smem, smem, smem, vmem, vmem, hbm, hbm],
        out_specs=(vmem, vmem),
        scratch_shapes=[
            pltpu.VMEM((f, tn), BF16),
            pltpu.VMEM((tn, f), BF16),
            pltpu.VMEM(weights.shape, BF16),
            pltpu.VMEM((slots, tile, tile), BF16),
            pltpu.VMEM((slots, tile, tile), BF16),
            pltpu.VMEM((nc, nd, f), BF16),
            pltpu.VMEM((relations * nt, nd, f), BF16),
            pltpu.VMEM((slots + 1, nd, f), F32),
            pltpu.VMEM((nk, nd, f), F32),
            pltpu.VMEM((nk, nd, f), F32),
            pltpu.VMEM((nk, nd, f), F32),
            pltpu.VMEM((16, 128), jnp.int32),
            pltpu.SMEM((16, 128), jnp.int32),
            pltpu.VMEM((2, 2, hop, 2 * q, f), BF16),
            pltpu.VMEM((2, 2, hop, 2 * q, f), BF16),
            pltpu.VMEM((2, 2, hop, q, f), BF16),
            pltpu.VMEM((2, 2, hop, q, f), BF16),
            pltpu.VMEM((nz, 2 * q, f), BF16),
            pltpu.VMEM((nz, 2 * q, f), BF16),
            pltpu.VMEM((2, 2 * q, f), BF16),
            pltpu.VMEM((relations, hb, nd, f), F32),
            pltpu.VMEM((relations, f, half), BF16),
            pltpu.VMEM((relations, nr - 1, prow, half), BF16),
            pltpu.VMEM((relations, prow, half), BF16),
            pltpu.VMEM((relations, nk, zrows, 128), BF16),
            dma(3), dma(SEMS), dma(SEMS),
        ],
        compiler_params=pltpu.CompilerParams(
            collective_id=0, has_side_effects=True, vmem_limit_bytes=67043328
        ),
    )(
        out_grad.T, node_in, tile_rows, tile_cols, tile_count.reshape(relations), tile_rows, tile_cols,
        weights, tile_vals.reshape(slots, tile, tile),
    )
    d_nodes, d_weights = widen(d_nodes, gathered)
    return d_nodes, d_weights.reshape(relations, f, f)


def solution(mesh):
    return jax.shard_map(
        functools.partial(body, mesh.shape["row"], mesh.shape["col"]),
        mesh=mesh,
        in_specs=(
            P("col", "row"),
            P(("row", "col"), None),
            P(),
            P(None, "col", "row", None, None, None),
            P(None, "col", "row", None),
            P(None, "col", "row", None),
            P(None, "col", "row"),
        ),
        out_specs=(P(("row", "col"), None), P()),
        check_vma=False,
    )
```

time: 182 us -> 97.6 us (0.54)
  Pallas kernels: 176 us -> 96.9 us
  local copies, waits for them, and re-layouts: 5.39 us -> 0 us
    pallas_call x2 -> x1, Pallas kernels: 173 us -> 94.1 us  [body(): pl.pallas_call(functools.partial(main_kernel, nr, nc, relations, cap), ou...]
    reshape x1 -> x0, local copies, waits for them, and re-layouts: 3.65 us -> none  [body(): d_nodes, d_weights = widen(d_nodes, gathered.reshape(relations * f, f))]
where the time goes in v1:
time: 97.6 us; the launch traced here: 97.5 us
  Pallas kernels  96.9 us (99%)
    pallas_call x1, Pallas kernels, body(): pl.pallas_call(functools.partial(main_kernel, nr, nc, relations, cap), ou...  94.1 us
    pallas_call x1, Pallas kernels, widen(): pl.pallas_call(widen_kernel, in_specs=[hbm, hbm], out_specs=(hbm, hbm), o...  2.8 us

profile of v1, /device:TPU:1, one launch (start us, length us, event | category | flops | bytes accessed | tf_op | source)
XLA Modules:
  0.0 97.5 jit_solution(3465250703479344359)
XLA Ops:
  0.6 94.1 %shard_map.86 = (bf16[128,512]{1,0:T(8,128)(2,1)}, bf16[1536,512]{1,0:T(8,128)(2,1)}) custom-call(bf16[64,1024]{1,0:T(8,128)(2,1)} %bitcast.5, bf16[128,512]{1,0:T(8,128)(2,1)} %nodes_ref.1, s32[3,1,1,32]{3,2,1,0:T(1,128)} %rows_v.1, s32[3,1,1,32]{3,2,1,0:T(1,128)} %cols_v.1, s32[3]{0:T(128)} %bitcast.6, s32[3,1,1,32]{3,2,1,0:T(1,128)} %rows_v.1, ...), custom_call_target="tpu_custom_call" | custom-call | tf_op jit(solution)/shard_map/pallas_call | solution.py:574
  94.7 2.8 %shard_map.87 = (bf16[128,512]{1,0:T(8,128)(2,1)}, f32[1536,512]{1,0:T(8,128)}) custom-call(bf16[128,512]{1,0:T(8,128)(2,1)} %get-tuple-element.6.dn_ref, bf16[1536,512]{1,0:T(8,128)(2,1)} %get-tuple-element.7.dw_ref), custom_call_target="tpu_custom_call" | custom-call | tf_op jit(solution)/shard_map/pallas_call | solution.py:538

commit v2 on v1

--- a/solution.py
+++ b/solution.py
@@ -228,7 +228,7 @@
             tilest[r * cap + s] = tiles[r * cap + s].T
             return carry
 
-        lax.fori_loop(0, cap, one, 0, unroll=4)
+        lax.fori_loop(0, cap, one, 0, unroll=16)
 
     turn(0)
     swap.wait_recv()
@@ -283,7 +283,7 @@
             acc[t + 1] = p + acc[link[r, s]]
             return carry
 
-        lax.fori_loop(0, cap, one, 0, unroll=4)
+        lax.fori_loop(0, cap, one, 0, unroll=16)
 
     mix(0)
     mix(1)
@@ -360,7 +360,7 @@
             acc[s + 1] = p + acc[link[4 + r, s]]
             return carry
 
-        lax.fori_loop(0, cap, one, 0, unroll=4)
+        lax.fori_loop(0, cap, one, 0, unroll=16)
         for i in range(nt):
             gy[i * nd : (i + 1) * nd, :] = acc[link[8 + r, i]].astype(BF16)
 
@@ -461,46 +461,55 @@
     n_round(1, a_names)
     for h in range(5, nz + 1):
         x_round(h)
+    for dz in rest:
+        n_core(dz)
     for c in sib:
         c.wait_recv()
+    near = [d for d in rest if abs(d) == nz // 2 - 2]
+    nearer = [d for d in rest if d not in near and d != 0]
+    last_cross = [d for d in rest if d not in near and d not in nearer]
     terms(0)
     product(0)
-    for dz in rest:
-        n_core(dz)
+    for dz in first:
+        n_cross(dz)
+    n_round(1, b_names)
     terms(1)
     product(1)
     plane_scatter(0)
-    for dz in first:
-        n_cross(dz)
-    n_round(1, b_names)
+    n_round(2, a_names)
     terms(2)
     product(2)
     plane_scatter(1)
-    for dz in rest:
+    plane_scatter(2)
+    for dz in near:
         n_cross(dz)
-    plane_scatter(2)
-    n_round(2, a_names)
     n_round(2, b_names)
+    n_round(3, a_names)
     for r in range(relations):
         z_scatter(r)
-    n_round(3, a_names)
-    n_round(3, b_names)
     for r in range(relations):
         z_gather(r)
+    for dz in nearer:
+        n_cross(dz)
+    n_round(3, b_names)
     for t in range(4, nz):
         n_round(t, a_names)
-        n_round(t, b_names)
     for r in range(relations):
         plane_gather(r)
     xf[0] = n_final("par").astype(BF16)
     xlast = send(xf.at[0], xf.at[1], xdev)
+    for dz in last_cross:
+        n_cross(dz)
+    for t in range(4, nz):
+        n_round(t, b_names)
+    core_gather(0)
+    core_gather(1)
     for st in b_names:
         dn_ref[x_rows(st), :] = n_final(st).astype(BF16)
     own = n_final("own")
     xlast.wait_recv()
     dn_ref[x_rows("own"), :] = (own + xf[1].astype(F32)).astype(BF16)
-    for r in range(relations):
-        core_gather(r)
+    core_gather(2)
     for c in last:
         c.wait_recv()
     for c in started:

time: 97.6 us -> 89.7 us (0.919)
  Pallas kernels: 96.9 us -> 88.8 us
    pallas_call x1, Pallas kernels: 94.1 us -> 86 us  [body(): pl.pallas_call(functools.partial(main_kernel, nr, nc, relations, cap), ou...]
where the time goes in v2:
time: 89.7 us; the launch traced here: 89.6 us
  Pallas kernels  88.8 us (99%)
    pallas_call x1, Pallas kernels, body(): pl.pallas_call(functools.partial(main_kernel, nr, nc, relations, cap), ou...  86 us
    pallas_call x1, Pallas kernels, widen(): pl.pallas_call(widen_kernel, in_specs=[hbm, hbm], out_specs=(hbm, hbm), o...  2.8 us

profile of v2, /device:TPU:1, one launch (start us, length us, event | category | flops | bytes accessed | tf_op | source)
XLA Modules:
  0.0 89.6 jit_solution(13614971603507090464)
XLA Ops:
  0.6 86.0 %shard_map.86 = (bf16[128,512]{1,0:T(8,128)(2,1)}, bf16[1536,512]{1,0:T(8,128)(2,1)}) custom-call(bf16[64,1024]{1,0:T(8,128)(2,1)} %bitcast.5, bf16[128,512]{1,0:T(8,128)(2,1)} %nodes_ref.1, s32[3,1,1,32]{3,2,1,0:T(1,128)} %rows_v.1, s32[3,1,1,32]{3,2,1,0:T(1,128)} %cols_v.1, s32[3]{0:T(128)} %bitcast.6, s32[3,1,1,32]{3,2,1,0:T(1,128)} %rows_v.1, ...), custom_call_target="tpu_custom_call" | custom-call | tf_op jit(solution)/shard_map/pallas_call | solution.py:583
  86.7 2.8 %shard_map.87 = (bf16[128,512]{1,0:T(8,128)(2,1)}, f32[1536,512]{1,0:T(8,128)}) custom-call(bf16[128,512]{1,0:T(8,128)(2,1)} %get-tuple-element.6.dn_ref, bf16[1536,512]{1,0:T(8,128)(2,1)} %get-tuple-element.7.dw_ref), custom_call_target="tpu_custom_call" | custom-call | tf_op jit(solution)/shard_map/pallas_call | solution.py:547

commit v3 on v2

--- a/solution.py
+++ b/solution.py
@@ -16,8 +16,8 @@
 def main_kernel(
     nr, nc, relations, cap,
     gin_ref, nodes_ref, rows_s, cols_s, count_s, rows_v, cols_v, w_hbm, t_hbm,
-    dn_ref, ag_ref,
-    gt, gy, w, tiles, tilest, xall, pm, acc, nsend, nrecv, nown, meta, link,
+    dn_out, ag_out,
+    dn_ref, ag_ref, gt, gy, w, tiles, tilest, xall, pm, acc, nsend, nrecv, nown, meta, link,
     zsa, zra, zsb, zrb, xs, xr, xf, dwrecv, pbuf, precv, zbuf, zrecv,
     load_sem, ssem, rsem,
 ):
@@ -433,19 +433,19 @@
         row = pl.multiple_of(r * f + who * prow, prow)
         return ag_ref.at[pl.ds(row, prow), pl.ds(pl.multiple_of(core * half, half), half)]
 
-    last = []
+    last = [[] for _ in range(relations)]
 
     def plane_gather(r):
         arrived(3, r)
         mine = strip(r, me_r)
         batches[4, r] = [send(mine, mine, row_peer(d)) for d in range(1, nr)]
-        last.append(send(mine, mine, sibling))
+        last[r].append(send(mine, mine, sibling))
 
     def core_gather(r):
         for d in range(1, nr):
             batches[4, r][d - 1].wait_recv()
             there = strip(r, lax.rem(me_r + nr - d, nr))
-            last.append(send(there, there, sibling))
+            last[r].append(send(there, there, sibling))
 
     first = [d for d in order if abs(d) >= nz // 2 - 1]
     rest = [d for d in order if d not in first]
@@ -510,8 +510,16 @@
     xlast.wait_recv()
     dn_ref[x_rows("own"), :] = (own + xf[1].astype(F32)).astype(BF16)
     core_gather(2)
-    for c in last:
-        c.wait_recv()
+    out = [pltpu.make_async_copy(dn_ref, dn_out, load_sem.at[3])]
+    out[0].start()
+    for r in range(relations):
+        for c in last[r]:
+            c.wait_recv()
+        block = pl.ds(r * f, f)
+        out.append(pltpu.make_async_copy(ag_ref.at[block, :], ag_out.at[block, :], load_sem.at[4 + r]))
+        out[-1].start()
+    for c in out:
+        c.wait()
     for c in started:
         c.wait_send()
     assert used[0] <= SEMS
@@ -587,8 +595,10 @@
             jax.ShapeDtypeStruct((relations * f, f), BF16),
         ),
         in_specs=[vmem, vmem, smem, smem, smem, vmem, vmem, hbm, hbm],
-        out_specs=(vmem, vmem),
+        out_specs=(hbm, hbm),
         scratch_shapes=[
+            pltpu.VMEM((nd, f), BF16),
+            pltpu.VMEM((relations * f, f), BF16),
             pltpu.VMEM((f, tn), BF16),
             pltpu.VMEM((tn, f), BF16),
             pltpu.VMEM(weights.shape, BF16),
@@ -614,7 +624,7 @@
             pltpu.VMEM((relations, nr - 1, prow, half), BF16),
             pltpu.VMEM((relations, prow, half), BF16),
             pltpu.VMEM((relations, nk, zrows, 128), BF16),
-            dma(3), dma(SEMS), dma(SEMS),
+            dma(4 + relations), dma(SEMS), dma(SEMS),
         ],
         compiler_params=pltpu.CompilerParams(
             collective_id=0, has_side_effects=True, vmem_limit_bytes=67043328

time: 89.7 us -> 89.4 us (level)
  no operation moved by 1% of the time
where the time goes in v3:
time: 89.4 us; the launch traced here: 89.3 us
  Pallas kernels  88.5 us (99%)
    pallas_call x1, Pallas kernels, body(): pl.pallas_call(functools.partial(main_kernel, nr, nc, relations, cap), ou...  85.7 us
    pallas_call x1, Pallas kernels, widen(): pl.pallas_call(widen_kernel, in_specs=[hbm, hbm], out_specs=(hbm, hbm), o...  2.8 us

profile of v3, /device:TPU:1, one launch (start us, length us, event | category | flops | bytes accessed | tf_op | source)
XLA Modules:
  0.0 89.3 jit_solution(8719956164817933237)
XLA Ops:
  0.6 85.7 %shard_map.86 = (bf16[128,512]{1,0:T(8,128)(2,1)}, bf16[1536,512]{1,0:T(8,128)(2,1)}) custom-call(bf16[64,1024]{1,0:T(8,128)(2,1)} %bitcast.5, bf16[128,512]{1,0:T(8,128)(2,1)} %nodes_ref.1, s32[3,1,1,32]{3,2,1,0:T(1,128)} %rows_v.1, s32[3,1,1,32]{3,2,1,0:T(1,128)} %cols_v.1, s32[3]{0:T(128)} %bitcast.6, s32[3,1,1,32]{3,2,1,0:T(1,128)} %rows_v.1, ...), custom_call_target="tpu_custom_call" | custom-call | tf_op jit(solution)/shard_map/pallas_call | solution.py:591
  86.3 2.8 %shard_map.87 = (bf16[128,512]{1,0:T(8,128)(2,1)}, f32[1536,512]{1,0:T(8,128)}) custom-call(bf16[128,512]{1,0:T(8,128)(2,1)} %get-tuple-element.6.dn_ref, bf16[1536,512]{1,0:T(8,128)(2,1)} %get-tuple-element.7.dw_ref), custom_call_target="tpu_custom_call" | custom-call | tf_op jit(solution)/shard_map/pallas_call | solution.py:555
